TPU v7x, 256 devices: a whole 4x4x8 slice. The times are simulated.
256 devices in a mesh: seq: 64 (over z, y, x_hi), tp: 4 (over x_lo, core).
Axes of the slice: x: 4 (x_hi: 2, x_lo: 2; x = x_hi * 2 + x_lo), y: 4, z: 8, core: 2. Of those that a mesh axis runs over, the one named last changes fastest.
Arguments:
- tokens: bfloat16 [32768, 2048], P('seq'), may hold values from -16 to 16
- forget: float32 [32768, 32], P('seq', 'tp'), may hold values from -5 to 0, as said below
- attn_gain: float32 [2048], replicated, may hold values from 0.1 to 1.9
- projections: bfloat16 [3, 2048, 2048], P(None, None, 'tp'), may hold values from -0.125 to 0.125
- out_weight: bfloat16 [2048, 2048], P('tp'), may hold values from -0.125 to 0.125
- ffn_gain: float32 [2048], replicated, may hold values from 0.1 to 1.9
- expand_weight: bfloat16 [2, 2048, 4096], P(None, None, 'tp'), may hold values from -0.125 to 0.125
- down_weight: bfloat16 [4096, 2048], P('tp'), may hold values from -0.09375 to 0.09375
Outputs:
- output: bfloat16 [32768, 2048], P('seq')
Inputs may be any that keep to these rules, and one draw needn't show every extreme that they name: forget is never positive.
All inputs are finite; a program needn't handle non-finite values.
Results may differ from a plain program's by a relative error of at most 0.011.
Values may be sent and summed in bfloat16 or wider, within the bound.
A program may use at most 128 MiB of HBM per device.

v0:
```python
import math

import jax
import jax.numpy as jnp
from jax import lax
from jax.sharding import Mesh
from jax.sharding import PartitionSpec as P

SEQ = ("seq_0", "seq_1", "seq_2")


norm_epsilon = 1e-05
head_epsilon = 1e-06


def filled_with(x, identity):
    return jax.tree.map(
        lambda a, e: jnp.broadcast_to(jnp.asarray(e, a.dtype), a.shape), x, identity
    )


def entering(x, axes, combine, identity):
    before = start = filled_with(x, identity)
    running = x
    for axis in reversed(axes):
        peers, index = (lax.axis_size(axis), lax.axis_index(axis))
        pieces = jax.tree.map(lambda part: lax.all_gather(part, axis), running)
        inside, running = (start, start)
        for k in range(peers):
            passed = k < index
            running = combine(running, jax.tree.map(lambda part: part[k], pieces))
            inside = jax.tree.map(lambda new, old: jnp.where(passed, new, old), running, inside)
        before = combine(inside, before)
    return before


def sent_to_all(x, axis):
    peers = lax.axis_size(axis)
    return lax.all_to_all(jnp.broadcast_to(x[None], (peers, *x.shape)), axis, 0, 0, tiled=True)


def joined_along(tiles, dim):
    tiles = jnp.moveaxis(tiles, 0, dim)
    dims = tiles.shape
    return tiles.reshape(*dims[:dim], dims[dim] * dims[dim + 1], *dims[dim + 2 :])


def gathered_copies(x, axis, dim):
    tiles = sent_to_all(x, axis)
    return joined_along(tiles, dim)


def in_blocks(x, dim, peers):
    dims = x.shape
    tiles = x.reshape(*dims[:dim], peers, dims[dim] // peers, *dims[dim + 1 :])
    return jnp.moveaxis(tiles, dim, 0)


def sum_at_owner(x, axis, dim):
    tiles = in_blocks(x, dim, lax.axis_size(axis))
    arrived = lax.all_to_all(tiles, axis, split_axis=0, concat_axis=0, tiled=True)
    return arrived.astype(jnp.float32).sum(axis=0)


def rms_scale(values, gain_vector):
    widened = values.astype(jnp.float32)
    mean_square = jnp.mean(widened * widened, axis=-1, keepdims=True)
    return (widened * lax.rsqrt(mean_square + norm_epsilon) * gain_vector).astype(jnp.bfloat16)


def summarize(key_rows, value_rows, forget_rows):
    log_decay = jnp.cumsum(forget_rows, axis=0)
    block_total = log_decay[-1]
    shrink_factors = jnp.exp(block_total[None, :] - log_decay)
    scaled_keys = (key_rows.astype(jnp.float32) * shrink_factors[:, :, None]).astype(jnp.bfloat16)
    block_state = jnp.einsum(
        "shd,she->hde", scaled_keys, value_rows, preferred_element_type=jnp.float32
    )
    return (log_decay, block_total, block_state)


def local_attention(query_rows, key_rows, value_rows, log_decay):
    head_size = query_rows.shape[2]
    score_scale = 1.0 / math.sqrt(head_size)
    scores = (
        jnp.einsum("thd,shd->hts", query_rows, key_rows, preferred_element_type=jnp.float32)
        * score_scale
    )
    log_gaps = log_decay.T[:, :, None] - log_decay.T[:, None, :]
    row_order = jnp.arange(query_rows.shape[0])
    causal = (row_order[:, None] >= row_order[None, :])[None]
    local_weights = jnp.where(
        causal, scores * jnp.exp(jnp.where(causal, log_gaps, 0.0)), 0.0
    ).astype(jnp.bfloat16)
    return jnp.einsum("hts,she->the", local_weights, value_rows, preferred_element_type=jnp.float32)


def finish_heads(query_rows, local_part, log_decay, incoming):
    head_size = query_rows.shape[2]
    score_scale = 1.0 / math.sqrt(head_size)
    carried = jnp.einsum(
        "thd,hde->the", query_rows.astype(jnp.float32), incoming, precision=lax.Precision.HIGHEST
    )
    attended = local_part + carried * (jnp.exp(log_decay) * score_scale)[:, :, None]
    mean_square = jnp.mean(attended * attended, axis=-1, keepdims=True)
    head_out = (attended * lax.rsqrt(mean_square + head_epsilon)).astype(jnp.bfloat16)
    return head_out.reshape(query_rows.shape[0], -1)


def feed_forward(rows_in, expand_weight):
    gate_proj = jnp.dot(rows_in, expand_weight[0], preferred_element_type=jnp.float32)
    up_proj = jnp.dot(rows_in, expand_weight[1], preferred_element_type=jnp.float32)
    return (jax.nn.silu(gate_proj) * up_proj).astype(jnp.bfloat16)


def local(tokens, forget, attn_gain, projections, out_weight, ffn_gain, expand_weight, down_weight):
    row_count = tokens.shape[0]
    head_count = forget.shape[1]
    head_size = projections.shape[2] // head_count
    normed = rms_scale(tokens, attn_gain)
    shaped = []
    for which in range(3):
        projected = jnp.dot(normed, projections[which], preferred_element_type=jnp.float32).astype(
            jnp.bfloat16
        )
        shaped.append(projected.reshape(row_count, head_count, head_size))
    query_rows, key_rows, value_rows = shaped
    log_decay, block_total, block_state = summarize(key_rows, value_rows, forget)

    def combine(earlier, following):
        return (earlier[0] * following[0], following[0][:, None, None] * earlier[1] + following[1])

    identity = (jnp.ones_like(block_total), jnp.zeros_like(block_state))
    _, incoming = entering((jnp.exp(block_total), block_state), SEQ, combine, identity)
    local_part = local_attention(query_rows, key_rows, value_rows, log_decay)
    head_out = finish_heads(query_rows, local_part, log_decay, incoming)
    row_share = row_count // lax.axis_size("tp")
    tp_index = lax.axis_index("tp")
    own_tokens = lax.dynamic_slice_in_dim(tokens, tp_index * row_share, row_share, 0)
    picked = head_out
    attn_summed = lax.psum_scatter(
        jnp.dot(picked, out_weight, preferred_element_type=jnp.float32).astype(jnp.bfloat16),
        "tp",
        scatter_dimension=0,
        tiled=True,
    ).astype(jnp.float32)
    residual = (own_tokens.astype(jnp.float32) + attn_summed).astype(jnp.bfloat16)
    normed_ffn = rms_scale(residual, ffn_gain)
    hidden = feed_forward(gathered_copies(normed_ffn, "tp", 0), expand_weight)
    picked = hidden
    ffn_summed = sum_at_owner(
        jnp.dot(picked, down_weight, preferred_element_type=jnp.float32).astype(jnp.bfloat16),
        "tp",
        0,
    )
    own_output = (residual.astype(jnp.float32) + ffn_summed).astype(jnp.bfloat16)
    return gathered_copies(own_output, "tp", 0)


def solution(mesh):
    torus = Mesh(mesh.devices.reshape(8, 4, 2, mesh.shape["tp"]), ("seq_0", "seq_1", "seq_2", "tp"))
    return jax.shard_map(
        local,
        mesh=torus,
        in_specs=(
            P(SEQ, None),
            P(SEQ, "tp"),
            P(),
            P(None, None, "tp"),
            P("tp", None),
            P(),
            P(None, None, "tp"),
            P("tp", None),
        ),
        out_specs=P(SEQ, None),
        check_vma=False,
    )
```

profile of v0, /device:TPU:1, one launch (start us, length us, event | category | flops | bytes accessed | tf_op | source)
XLA Modules:
  0.0 250.8 jit_solution(8597326125596798398)
XLA Ops:
  6.5 0.0 copy-start
  6.5 0.0 all-gather.6.cloned.1.call-start
  6.5 2.2 fusion
  8.8 0.0 copy-done.8
  8.8 0.1 copy-done.1
  8.9 3.0 %fusion.33 = bf16[512,512]{0,1:T(8,128)(2,1)S(1)} fusion(bf16[3,2048,512]{2,1,0:T(8,128)(2,1)} %param.11, bf16[512,2048]{1,0:T(8,128)(2,1)S(1)} %copy-done.1, f32[2048]{0:T(1024)S(1)} %copy-done.8, f32[512]{0:T(512)S(1)} %add_rsqrt_fusion.1), kind=kOutput, calls=%fused_computation.37 | convolution fusion | flops 1078198272 | bytes 4728832 | tf_op jit(solution)/shard_map/dot_general | solution.py:123
  12.0 0.0 copy-start.6
  12.0 3.2 %fusion.27 = bf16[512,512]{0,1:T(8,128)(2,1)S(1)} fusion(bf16[3,2048,512]{2,1,0:T(8,128)(2,1)} %param.11, bf16[512,2048]{1,0:T(8,128)(2,1)S(1)} %copy-done.1, f32[2048]{0:T(1024)S(1)} %copy-done.8, f32[512]{0:T(512)S(1)} %add_rsqrt_fusion.1), kind=kOutput, calls=%fused_computation.35 | convolution fusion | flops 1078198272 | bytes 4728832 | tf_op jit(solution)/shard_map/dot_general | solution.py:123
  15.2 1.1 reduce-window.6
  16.4 0.2 slice_reduce_fusion
  16.6 0.1 exponential_multiply_fusion
  16.7 0.2 exponential_reduce_fusion
  16.9 0.1 subtract_exponential_fusion
  16.9 5.2 %all-gather.1 = f32[2,1,8]{2,1,0:T(1,128)S(1)} all-gather(f32[1,1,8]{2,1,0:T(1,128)S(1)} %bitcast.234), channel_id=1, replica_groups=mesh['seq_0'=8,'seq_1'=4,'seq_2'=2,'tp'=4] {'seq_2'}, dimensions={0}, use_global_device_ids=true | all-gather | bytes 96 | tf_op jit(solution)/shard_map/all_gather | solution.py:27
  22.1 8.2 %all-gather.2 = f32[4,1,8]{2,1,0:T(1,128)S(1)} all-gather(f32[1,1,8]{2,1,0:T(1,128)S(1)} %get-tuple-element.27), channel_id=1, replica_groups=mesh['seq_0'=8,'seq_1'=4,'seq_2'=2,'tp'=4] {'seq_1'}, dimensions={0}, use_global_device_ids=true | all-gather | bytes 160 | tf_op jit(solution)/shard_map/all_gather | solution.py:27
  30.3 0.3 fusion.43
  30.6 7.4 %all-gather = f32[16,64,64]{2,1,0:T(8,128)S(1)} all-gather(f32[8,64,64]{2,1,0:T(8,128)S(1)} %fusion.43), channel_id=2, replica_groups=mesh['seq_0'=8,'seq_1'=4,'seq_2'=2,'tp'=4] {'seq_2'}, dimensions={0}, use_global_device_ids=true | all-gather | bytes 393216 | tf_op jit(solution)/shard_map/all_gather | solution.py:27
  38.0 0.8 copy-done.2
  38.8 0.1 bitcast_add_fusion.4
  38.9 12.5 %all_gather.31 = f32[4,8,64,64]{3,2,1,0:T(8,128)S(1)} all-gather(f32[1,8,64,64]{3,2,1,0:T(8,128)S(1)} %bitcast_add_fusion.4), channel_id=1, replica_groups=mesh['seq_0'=8,'seq_1'=4,'seq_2'=2,'tp'=4] {'seq_1'}, dimensions={0}, use_global_device_ids=true | all-gather | bytes 655360 | tf_op jit(solution)/shard_map/all_gather | solution.py:27
  51.3 0.8 multiply_add_fusion
  52.2 0.0 all-gather.6.cloned.1.call-update
  52.2 0.0 reduce-scatter.2.cloned.1.call-start
  52.2 15.9 %all-gather.3 = f32[8,1,8]{2,1,0:T(1,128)S(1)} all-gather(f32[1,1,8]{2,1,0:T(1,128)S(1)} %get-tuple-element.21), channel_id=1, replica_groups=mesh['seq_0'=8,'seq_1'=4,'seq_2'=2,'tp'=4] {'seq_0'}, dimensions={0}, use_global_device_ids=true | all-gather | bytes 288 | tf_op jit(solution)/shard_map/all_gather | solution.py:27
  68.1 0.1 iota_compare_fusion
  68.2 0.1 add_bitcast_fusion.1
  68.3 4.4 %fusion.30 = bf16[512,512]{0,1:T(8,128)(2,1)} fusion(bf16[3,2048,512]{2,1,0:T(8,128)(2,1)} %param.11, bf16[512,2048]{1,0:T(8,128)(2,1)} %param.8, f32[2048]{0:T(1024)S(1)} %copy-done.8, f32[512]{0:T(512)S(1)} %add_rsqrt_fusion.1), kind=kOutput, calls=%fused_computation.36 | convolution fusion | flops 1078198272 | bytes 4728832 | tf_op jit(solution)/shard_map/dot_general | solution.py:123
  72.7 6.3 %fusion.24 = f32[512,8,64]{0,2,1:T(8,128)} fusion(bf16[512,8,64]{0,2,1:T(8,128)(2,1)} %bitcast.232, f32[8,512]{1,0:T(8,128)S(1)} %add_bitcast_fusion.1, pred[512,512]{1,0:T(8,128)(4,1)S(1)} %iota_compare_fusion, bf16[512,8,64]{0,2,1:T(8,128)(2,1)} %bitcast.235, bf16[512,8,64]{0,2,1:T(8,128)(2,1)} %bitcast.230), kind=kOutput, calls=%fused_computation.31 | convolution fusion | flops 549453824 | bytes 2899968 | tf_op jit(solution)/shard_map/hts,she->the/dot_general | solution.py:95
  79.0 18.2 %all-gather.6.cloned.1.call-done = f32[8,8,64,64]{3,2,1,0:T(8,128)} async-done(((f32[1,8,64,64]{3,2,1,0:T(8,128)}), f32[8,8,64,64]{3,2,1,0:T(8,128)}) %all-gather.6.cloned.1.call-update) | async-done | bytes 1048592 | tf_op jit(solution)/shard_map/all_gather | solution.py:27
  97.2 3.4 %multiply_reduce_fusion = (f32[512,8]{0,1:T(8,128)S(1)}, f32[512,8,64]{0,2,1:T(8,128)S(1)}) fusion(f32[512,8,64]{0,2,1:T(8,128)} %fusion.24, f32[512,8]{0,1:T(8,128)S(1)} %get-tuple-element.11, bf16[512,8,64]{0,2,1:T(8,128)(2,1)} %bitcast.236, f32[8,8,64,64]{3,2,1,0:T(8,128)} %all-gather.6.cloned.1.call-done, f32[4,8,64,64]{3,2,1,0:T(8,128)S(1)} %all_gather.31, ...), kind=kOutput, calls=%fused_computation.45 | convolution fusion | flops 203780096 | bytes 4489742 | tf_op jit(solution)/shard_map/thd,hde->the/dot_general | solution.py:101
  100.6 0.1 multiply_convert_fusion.1
  100.8 0.0 copy-done
  100.8 2.6 %convolution_convert_fusion.1 = bf16[512,2048]{1,0:T(8,128)(2,1)} fusion(bf16[512,512]{0,1:T(8,128)(2,1)S(1)} %bitcast.228, bf16[512,2048]{1,0:T(8,128)(2,1)S(1)} %copy-done), kind=kOutput, calls=%fused_computation.17 | convolution fusion | flops 1074790400 | bytes 4718592 | tf_op jit(solution)/shard_map/dot_general | solution.py:142
  103.4 0.0 reduce-scatter.2.cloned.1.call-update
  103.4 33.9 %reduce-scatter.2.cloned.1.call-done = bf16[128,2048]{1,0:T(8,128)(2,1)} async-done(((bf16[512,2048]{1,0:T(8,128)(2,1)}), bf16[128,2048]{1,0:T(8,128)(2,1)}) %reduce-scatter.2.cloned.1.call-update) | async-done | bytes 524304 | tf_op jit(solution)/shard_map/reduce_scatter | solution.py:141
  137.3 1.5 fusion.38
  138.8 0.2 fusion.40
  139.0 0.2 broadcast_in_dim.56
  139.2 27.4 %all_to_all.15 = bf16[4,128,2048]{2,1,0:T(8,128)(2,1)S(1)} all-to-all(bf16[4,128,2048]{2,1,0:T(8,128)(2,1)S(1)} %broadcast_in_dim.56), channel_id=1, replica_groups=mesh['seq_0'=8,'seq_1'=4,'seq_2'=2,'tp'=4] {'tp'}, dimensions={0} | all-to-all | bytes 4194304 | tf_op jit(solution)/shard_map/all_to_all | solution.py:39
  166.7 1.3 copy-done.3
  168.0 5.9 %fusion.5 = f32[512,1024]{1,0:T(8,128)} fusion(bf16[512,2048]{1,0:T(8,128)(2,1)S(1)} %bitcast.225, bf16[2,2048,1024]{2,1,0:T(8,128)(2,1)} %param.14), kind=kOutput, calls=%fused_computation.8 | convolution fusion | flops 2147483648 | bytes 8388608 | tf_op jit(solution)/shard_map/dot_general | solution.py:111
  173.9 10.5 %convolution_convert_fusion = bf16[512,2048]{1,0:T(8,128)(2,1)} fusion(bf16[1024,2048]{1,0:T(8,128)(2,1)} %param.15, f32[512,1024]{1,0:T(8,128)} %fusion.5, bf16[512,2048]{1,0:T(8,128)(2,1)} %bitcast.226, bf16[2,2048,1024]{2,1,0:T(8,128)(2,1)} %param.14), kind=kOutput, calls=%fused_computation.16 | convolution fusion | flops 4299161600 | bytes 14680064 | tf_op jit(solution)/shard_map/dot_general | solution.py:152
  184.4 29.2 %all_to_all.16 = bf16[4,128,2048]{2,1,0:T(8,128)(2,1)S(1)} all-to-all(bf16[4,128,2048]{2,1,0:T(8,128)(2,1)} %bitcast.227), channel_id=1, replica_groups=mesh['seq_0'=8,'seq_1'=4,'seq_2'=2,'tp'=4] {'tp'}, dimensions={0} | all-to-all | bytes 4194304 | tf_op jit(solution)/shard_map/all_to_all | solution.py:61
  213.7 0.4 convert_reduce_fusion
  214.1 0.1 fusion.41
  214.2 0.3 broadcast_in_dim.57
  214.5 28.1 %all_to_all.17 = bf16[4,128,2048]{2,1,0:T(8,128)(2,1)S(1)} all-to-all(bf16[4,128,2048]{2,1,0:T(8,128)(2,1)S(1)} %broadcast_in_dim.57), channel_id=1, replica_groups=mesh['seq_0'=8,'seq_1'=4,'seq_2'=2,'tp'=4] {'tp'}, dimensions={0} | all-to-all | bytes 4194304 | tf_op jit(solution)/shard_map/all_to_all | solution.py:39
  242.6 1.3 copy.19
  (20 shorter events, 0.1 us)
Async XLA Ops:
  6.5 94.3 %copy-start = (bf16[512,2048]{1,0:T(8,128)(2,1)S(1)}, bf16[512,2048]{1,0:T(8,128)(2,1)}, u32[]{:S(2)}) copy-start(bf16[512,2048]{1,0:T(8,128)(2,1)} %param.12) | copy-start | bytes 6291460
  6.5 2.2 copy-start.8
  6.5 90.6 %all-gather.6.cloned.1.call-start = ((), (), s32[]{:S(2)}) async-start(), calls=%async_computation.4 | async-start | bytes 2359296 | tf_op jit(solution)/shard_map/all_gather | solution.py:27
  6.5 2.4 copy-start.1
  12.0 18.3 %copy-start.4 = (bf16[512,512]{0,1:T(8,128)(2,1)}, bf16[512,512]{0,1:T(8,128)(2,1)S(1)}, u32[]{:S(2)}) copy-start(bf16[512,512]{0,1:T(8,128)(2,1)S(1)} %fusion.33) | copy-start | bytes 1572868
  12.0 3.3 %copy-start.6 = (f32[512,8]{0,1:T(8,128)S(1)}, f32[512,8]{0,1:T(8,128)}, u32[]{:S(2)}) copy-start(f32[512,8]{0,1:T(8,128)} %param.9) | copy-start | bytes 49156
  15.2 22.8 %copy-start.5 = (bf16[512,512]{0,1:T(8,128)(2,1)}, bf16[512,512]{0,1:T(8,128)(2,1)S(1)}, u32[]{:S(2)}) copy-start(bf16[512,512]{0,1:T(8,128)(2,1)S(1)} %fusion.27) | copy-start | bytes 1572868
  38.0 0.8 copy-start.2
  52.2 85.1 %reduce-scatter.2.cloned.1.call-start = ((), (), s32[]{:S(2)}) async-start(), calls=%async_computation.5 | async-start | bytes 2621440 | tf_op jit(solution)/shard_map/reduce_scatter | solution.py:141
  103.4 35.4 %copy-start.7 = (f32[2048]{0:T(1024)S(1)}, f32[2048]{0:T(1024)}, u32[]{:S(2)}) copy-start(f32[2048]{0:T(1024)} %param.13) | copy-start | bytes 24580
  166.7 1.4 copy-start.3
Sparse Core Ops, SparseCore 0:
  52.3 44.8 all-gather.5
  103.5 33.7 reduce-scatter.1
where the time goes:
time: 251 us
  blocking collectives  134 us (53%)
  waiting for transfers between devices  52.1 us (21%)
  matrix products  39.7 us (16%)
  between operations  13.6 us (5%)
  other arithmetic  7 us (3%)
  local copies, waits for them, and re-layouts  4.47 us (2%)
    all_to_all x2, blocking collectives, sent_to_all(): lax.all_to_all(jnp.broadcast_to(x[None], (peers, *x.shape)), axis, 0, 0,...  55.6 us
    all_gather x5, blocking collectives, entering(): pieces = jax.tree.map(lambda part: lax.all_gather(part, axis), running)  49.1 us
    reduce_scatter x1, waiting for transfers between devices, local(): lax.psum_scatter(jnp.dot(picked, out_weight, preferred_element_type=jnp.f...  33.9 us
    all_to_all x1, blocking collectives, sum_at_owner(): lax.all_to_all(tiles, axis, split_axis=0, concat_axis=0, tiled=True)  29.2 us
    all_gather x1, waiting for transfers between devices, entering(): pieces = jax.tree.map(lambda part: lax.all_gather(part, axis), running)  18.2 us
    dot_general x3, matrix products, local(): jnp.dot(normed, projections[which], preferred_element_type=jnp.float32)  10.6 us
    dot_general x1, matrix products, local(): jnp.dot(picked, down_weight, preferred_element_type=jnp.float32)  10.5 us
    dot_general x1, matrix products, local_attention(): jnp.einsum('hts,she->the', local_weights, value_rows, preferred_element_t...  6.32 us
  transfers between devices with their start and end apart: 2, of which 2 were waited for; matrix products, arithmetic and copies ran while one was open for 4% of the time, Pallas kernels for 0%

commit v1 on v0

v1 whole, which is shorter than its diff:
```python
import functools

import jax
import jax.numpy as jnp
from jax import lax
from jax.experimental import pallas as pl
from jax.experimental.pallas import tpu as pltpu
from jax.sharding import PartitionSpec as P

MESH = pl.DeviceIdType.MESH
F32 = jnp.float32
BF16 = jnp.bfloat16

norm_epsilon = 1e-05
head_epsilon = 1e-06

TOK = 512
D = 2048
HD = 512
FF = 1024
CH = 4
RW = TOK // CH
OW = RW // 4
NP = 4
PLANE = 8
DEPTH = 8


def dot(a, b):
    return jnp.dot(a, b, preferred_element_type=F32)


def kernel(
    tok_h, forget_h, again_h, proj_h, outw_h, fgain_h, exp_h, down_h, out_h,
    tok, fgt, again, fgain, proj, outw, wexp, wdown,
    normed, qs, ks, vs, ld, ldt, ldx, local,
    ldsend, ld_in, ltsend, lt_in, ssend, s_in, pref, tsend, t_in, isend, i_in, inc,
    ho, psend, prec, pk, pisend, pirec,
    resid, xrows, hidden, ysend, yrec, yk, yisend, yirec, out,
    tok_sem, w_sem, out_sem,
    ld_ss, ld_rs, lt_ss, lt_rs, s_ss, s_rs, t_ss, t_rs, i_ss, i_rs,
    p_ss, p_rs, pi_ss, pi_rs, xd_ss, xd_rs, xi_ss, xi_rs, xf_ss, xf_rs,
    y_ss, y_rs, yi_ss, yi_rs, od_ss, od_rs, oi_ss, oi_rs, of_ss, of_rs,
):
    s = lax.axis_index("seq")
    t = lax.axis_index("tp")
    plane = lax.rem(s, PLANE)
    z = s // PLANE
    c = t // 2
    k = lax.rem(t, 2)
    core_peer = (s, c * 2 + (1 - k))
    chip_peer = (s, (1 - c) * 2 + k)
    ffn_peer = (s + 1 - 2 * lax.rem(s, 2), (1 - c) * 2 + k)

    def plane_peer(d):
        j = lax.rem(plane + d, PLANE)
        return j, (z * PLANE + j, t)

    def depth_peer(d):
        j = lax.rem(z + d, DEPTH)
        return j, (j * PLANE + plane, t)

    def remote(src, dst, ssem, rsem, dev):
        return pltpu.make_async_remote_copy(
            src_ref=src, dst_ref=dst, send_sem=ssem, recv_sem=rsem,
            device_id=dev, device_id_type=MESH,
        )

    barrier = pltpu.get_barrier_semaphore()
    for d in range(1, PLANE):
        pl.semaphore_signal(barrier, inc=1, device_id=plane_peer(d)[1], device_id_type=MESH)
    for d in range(1, DEPTH):
        pl.semaphore_signal(barrier, inc=1, device_id=depth_peer(d)[1], device_id_type=MESH)
    for dev in (core_peer, chip_peer, ffn_peer):
        pl.semaphore_signal(barrier, inc=1, device_id=dev, device_id_type=MESH)

    def tok_copy(i):
        rows = pl.ds(i * RW, RW)
        return pltpu.make_async_copy(tok_h.at[rows], tok.at[rows], tok_sem.at[i])

    for i in range(CH):
        tok_copy(i).start()
    forget_copy = pltpu.make_async_copy(forget_h, fgt, w_sem.at[0])
    again_copy = pltpu.make_async_copy(again_h, again, w_sem.at[1])
    proj_copies = [
        pltpu.make_async_copy(proj_h.at[w], proj.at[w], w_sem.at[2 + w]) for w in range(3)
    ]
    fgain_copy = pltpu.make_async_copy(fgain_h, fgain, w_sem.at[5])
    outw_copy = pltpu.make_async_copy(outw_h, outw, w_sem.at[6])
    exp_copy = pltpu.make_async_copy(exp_h, wexp, w_sem.at[7])
    down_copy = pltpu.make_async_copy(down_h, wdown, w_sem.at[8])
    forget_copy.start()
    again_copy.start()
    proj_copies[1].start()
    proj_copies[2].start()

    forget_copy.wait()
    f = fgt[...]
    f1 = f.astype(BF16)
    rest = f - f1.astype(F32)
    f2 = rest.astype(BF16)
    f3 = (rest - f2.astype(F32)).astype(BF16)
    row_at = lax.broadcasted_iota(jnp.int32, (TOK, TOK), 0)
    col_at = lax.broadcasted_iota(jnp.int32, (TOK, TOK), 1)
    lower = jnp.where(row_at >= col_at, 1.0, 0.0).astype(BF16)
    sums = dot(lower, f1) + (dot(lower, f2) + dot(lower, f3))
    ld[:, 0:8] = sums
    ld[:, 8:128] = jnp.zeros((TOK, 120), F32)
    turned = jnp.transpose(ld[...])
    for h in range(8):
        ldt[h] = turned[h : h + 1]
    total = jnp.broadcast_to(turned[0:8, TOK - 1 : TOK], (8, 128))
    ldsend[...] = total
    ld_in[plane] = total

    low_lanes = lax.broadcasted_iota(jnp.int32, (RW, 128), 1) < 64
    for i in range(CH):
        for p in range(NP):
            rows = slice(i * RW, (i + 1) * RW)
            ldx[rows, p * 128 : (p + 1) * 128] = jnp.where(
                low_lanes, ld[rows, 2 * p : 2 * p + 1], ld[rows, 2 * p + 1 : 2 * p + 2]
            )

    again_copy.wait()

    def norm_rows(i, _):
        pltpu.make_async_copy(
            tok_h.at[pl.ds(i * RW, RW)], tok.at[pl.ds(i * RW, RW)], tok_sem.at[i]
        ).wait()
        rows = pl.ds(pl.multiple_of(i * RW, RW), RW)
        x = tok[rows, :].astype(F32)
        mean_square = jnp.sum(x * x, axis=1, keepdims=True) * (1.0 / D)
        scale = lax.rsqrt(mean_square + norm_epsilon)
        normed[rows, :] = (tok[rows, :].astype(F32) * scale * again[...]).astype(BF16)
        return _

    lax.fori_loop(0, CH, norm_rows, 0)

    proj_copies[0].start()
    fgain_copy.start()
    outw_copy.start()
    exp_copy.start()
    down_copy.start()

    pl.semaphore_wait(barrier, PLANE - 1 + DEPTH - 1 + 3)
    for d in range(1, PLANE):
        j, dev = plane_peer(d)
        remote(ldsend, ld_in.at[plane], ld_ss.at[d], ld_rs.at[d], dev).start()

    proj_copies[1].wait()
    ks[...] = dot(normed[...], proj[1]).astype(BF16)
    proj_copies[2].wait()
    vs[...] = dot(normed[...], proj[2]).astype(BF16)

    lanes32 = lax.broadcasted_iota(jnp.int32, (32, 128), 1) < 64
    for p in range(NP):
        cols = slice(p * 128, (p + 1) * 128)
        decay = jnp.exp(ldx[TOK - 1 : TOK, cols] - ldx[:, cols])
        scaled = (ks[:, cols].astype(F32) * decay).astype(BF16)
        m = lax.dot_general(
            scaled, vs[:, cols], (((0,), (0,)), ((), ())), preferred_element_type=F32
        )
        even = jnp.where(lanes32, m[0:32], pltpu.roll(m[32:64], 64, 1))
        odd = jnp.where(lanes32, pltpu.roll(m[64:96], 64, 1), m[96:128])
        ssend[2 * p] = even.astype(BF16)
        ssend[2 * p + 1] = odd.astype(BF16)

    s_in[plane] = ssend[plane]
    for d in range(1, PLANE):
        j, dev = plane_peer(d)
        remote(ssend.at[j], s_in.at[plane], s_ss.at[d], s_rs.at[d], dev).start()

    for d in range(1, PLANE):
        remote(ldsend, ld_in.at[0], ld_ss.at[d], ld_rs.at[d], core_peer).wait_recv()
    plane_total = ld_in[0]
    for j in range(1, PLANE):
        plane_total = plane_total + ld_in[j]
    ltsend[...] = plane_total
    lt_in[z] = plane_total
    for d in range(1, DEPTH):
        j, dev = depth_peer(d)
        remote(ltsend, lt_in.at[z], lt_ss.at[d], lt_rs.at[d], dev).start()

    proj_copies[0].wait()
    qs[...] = (dot(normed[...], proj[0]) * 0.125).astype(BF16)

    def send_totals():
        for d in range(1, PLANE):
            remote(ssend.at[0], s_in.at[0], s_ss.at[d], s_rs.at[d], core_peer).wait_recv()
        state = jnp.zeros((32, 128), F32)
        for j in range(PLANE):
            pref[j] = state
            state = jnp.exp(ld_in[j, pl.ds(plane, 1), :]) * state + s_in[j].astype(F32)
        rounded = state.astype(BF16)
        tsend[...] = rounded
        t_in[z] = rounded
        for d in range(1, DEPTH):
            j, dev = depth_peer(d)
            remote(tsend, t_in.at[z], t_ss.at[d], t_rs.at[d], dev).start()

    def send_prefixes():
        for d in range(1, DEPTH):
            remote(ltsend, lt_in.at[0], lt_ss.at[d], lt_rs.at[d], core_peer).wait_recv()
            remote(tsend, t_in.at[0], t_ss.at[d], t_rs.at[d], core_peer).wait_recv()
        state = jnp.zeros((32, 128), F32)
        for j in range(DEPTH):
            following = jnp.exp(lt_in[j, pl.ds(plane, 1), :]) * state + t_in[j].astype(F32)
            state = jnp.where(j < z, following, state)
        passed = jnp.zeros((1, 128), F32)
        for j in range(PLANE):
            isend[j] = (pref[j] + jnp.exp(passed) * state).astype(BF16)
            passed = passed + ld_in[j, pl.ds(plane, 1), :]
        i_in[plane] = isend[plane]
        for d in range(1, PLANE):
            j, dev = plane_peer(d)
            remote(isend.at[j], i_in.at[plane], i_ss.at[d], i_rs.at[d], dev).start()

    lanes512 = lax.broadcasted_iota(jnp.int32, (TOK, 128), 1) < 64
    causal = lax.broadcasted_iota(jnp.int32, (RW, RW), 0) >= lax.broadcasted_iota(
        jnp.int32, (RW, RW), 1
    )
    zero = jnp.zeros((), BF16)

    def pair_step(p, _):
        cols = pl.ds(pl.multiple_of(p * 128, 128), 128)
        kp = ks[:, cols]
        vp = vs[:, cols]
        for h in range(2):
            mine = lanes512 if h == 0 else jnp.logical_not(lanes512)
            vh = jnp.where(mine, vp.astype(F32), 0.0).astype(BF16)
            for i in range(CH):
                rows = slice(i * RW, (i + 1) * RW)
                span = (i + 1) * RW
                qh = jnp.where(mine[0:RW], qs[rows, cols].astype(F32), 0.0).astype(BF16)
                scores = lax.dot_general(
                    qh, kp[0:span], (((1,), (1,)), ((), ())), preferred_element_type=F32
                )
                here = ldx[rows, cols][:, 64 * h : 64 * h + 1]
                there = ldt[2 * p + h]
                parts = []
                for b in range(i + 1):
                    gap = here - there[:, b * RW : (b + 1) * RW]
                    if b == i:
                        gap = jnp.where(causal, gap, -1e30)
                    parts.append(
                        (scores[:, b * RW : (b + 1) * RW] * jnp.exp(gap)).astype(BF16)
                    )
                weights = parts[0] if i == 0 else jnp.concatenate(parts, axis=1)
                part = dot(weights, vh[0:span])
                if h == 0:
                    local[rows, cols] = part
                else:
                    local[rows, cols] = local[rows, cols] + part

        @pl.when(p == 1)
        def _totals():
            send_totals()

        @pl.when(p == 3)
        def _prefixes():
            send_prefixes()

        return _

    lax.fori_loop(0, NP, pair_step, 0)

    for d in range(1, PLANE):
        remote(isend.at[0], i_in.at[0], i_ss.at[d], i_rs.at[d], core_peer).wait_recv()
    for p in range(NP):
        even = i_in[2 * p].astype(F32)
        odd = i_in[2 * p + 1].astype(F32)
        inc[p, 0:32, :] = jnp.where(lanes32, even, 0.0).astype(BF16)
        inc[p, 32:64, :] = jnp.where(lanes32, pltpu.roll(even, 64, 1), 0.0).astype(BF16)
        inc[p, 64:96, :] = jnp.where(lanes32, 0.0, pltpu.roll(odd, 64, 1)).astype(BF16)
        inc[p, 96:128, :] = jnp.where(lanes32, 0.0, odd).astype(BF16)

    same_head = jnp.where(
        (lax.broadcasted_iota(jnp.int32, (128, 128), 0) < 64)
        == (lax.broadcasted_iota(jnp.int32, (128, 128), 1) < 64),
        1.0,
        0.0,
    ).astype(BF16)

    def partial_to_core(i):
        return remote(psend.at[i], prec.at[i], p_ss.at[i], p_rs.at[i], core_peer)

    def partial_to_chip(i):
        return remote(pisend.at[i], pirec.at[i], pi_ss.at[i], pi_rs.at[i], chip_peer)

    def stage_a(i):
        rows = pl.ds(pl.multiple_of(i * RW, RW), RW)
        for p in range(NP):
            cols = slice(p * 128, (p + 1) * 128)
            carried = dot(qs[rows, cols], inc[p])
            attended = local[rows, cols] + carried * jnp.exp(ldx[rows, cols])
            square = attended * attended
            high = square.astype(BF16)
            low = (square - high.astype(F32)).astype(BF16)
            mean_square = (dot(high, same_head) + dot(low, same_head)) * (1.0 / 64)
            headed = (attended * lax.rsqrt(mean_square + head_epsilon)).astype(BF16)
            for kk in range(2):
                core_slot = 1 - k if kk == 0 else k
                for cc in range(2):
                    chip_slot = c if cc == 0 else 1 - c
                    at = pl.multiple_of(core_slot * 2 * OW + chip_slot * OW, OW)
                    ho[pl.ds(at, OW), cols] = headed[(kk * 2 + cc) * OW : (kk * 2 + cc + 1) * OW]
        for n in range(4):
            cols = slice(n * 512, (n + 1) * 512)
            part = dot(ho[...], outw[:, cols])
            psend[i, :, cols] = part[0 : 2 * OW].astype(BF16)
            pk[i, :, cols] = part[2 * OW : 4 * OW]
        partial_to_core(i).start()

    def stage_b(i):
        partial_to_core(i).wait_recv()
        pisend[i] = (pk[i, OW : 2 * OW, :] + prec[i, OW : 2 * OW, :].astype(F32)).astype(BF16)
        partial_to_chip(i).start()

    own_at = k * 2 * OW + c * OW

    def rows_to_core(i):
        return remote(
            xrows.at[i, pl.ds(2 * OW, OW)], xrows.at[i, pl.ds(0, OW)],
            xd_ss.at[i], xd_rs.at[i], core_peer,
        )

    def rows_to_ffn(i):
        return remote(
            xrows.at[i, pl.ds(2 * OW, OW)], xrows.at[i, pl.ds(3 * OW, OW)],
            xi_ss.at[i], xi_rs.at[i], ffn_peer,
        )

    def rows_forward(i):
        return remote(
            xrows.at[i, pl.ds(3 * OW, OW)], xrows.at[i, pl.ds(OW, OW)],
            xf_ss.at[i], xf_rs.at[i], core_peer,
        )

    def stage_c(i):
        partial_to_chip(i).wait_recv()
        rows = pl.ds(pl.multiple_of(i * RW + own_at, OW), OW)
        res = (
            tok[rows, :].astype(F32)
            + (pk[i, 0:OW, :] + prec[i, 0:OW, :].astype(F32) + pirec[i].astype(F32))
        ).astype(BF16)
        resid[i] = res
        wide = res.astype(F32)
        mean_square = jnp.sum(wide * wide, axis=1, keepdims=True) * (1.0 / D)
        scale = lax.rsqrt(mean_square + norm_epsilon)
        xrows[i, 2 * OW : 3 * OW, :] = (wide * scale * fgain[...]).astype(BF16)
        rows_to_ffn(i).start()
        rows_to_core(i).start()

    def stage_d(i):
        rows_to_ffn(i).wait_recv()
        rows_forward(i).start()

    def sums_to_core(i):
        return remote(ysend.at[i], yrec.at[i], y_ss.at[i], y_rs.at[i], core_peer)

    def sums_to_ffn(i):
        return remote(yisend.at[i], yirec.at[i], yi_ss.at[i], yi_rs.at[i], ffn_peer)

    def stage_e_expand(i):
        rows_to_core(i).wait_recv()
        rows_forward(i).wait_recv()
        x = xrows.at[i]
        for n in range(4):
            cols = slice(n * 256, (n + 1) * 256)
            gate = dot(x[...], wexp[0, :, cols])
            up = dot(x[...], wexp[1, :, cols])
            hidden[:, cols] = (gate / (1.0 + jnp.exp(-gate)) * up).astype(BF16)

    def stage_e_down(i):
        for n in range(4):
            cols = slice(n * 512, (n + 1) * 512)
            part = dot(hidden[...], wdown[:, cols])
            ysend[i, :, cols] = part[0 : 2 * OW].astype(BF16)
            yk[i, :, cols] = part[2 * OW : 4 * OW]
        sums_to_core(i).start()

    def stage_f(i):
        sums_to_core(i).wait_recv()
        yisend[i] = (yk[i, OW : 2 * OW, :] + yrec[i, OW : 2 * OW, :].astype(F32)).astype(BF16)
        sums_to_ffn(i).start()

    own_rows = pl.ds(pl.multiple_of(own_at, OW), OW)
    chip_rows = pl.ds(pl.multiple_of(k * 2 * OW + (1 - c) * OW, OW), OW)

    def out_to_core(i):
        return remote(
            out.at[i, own_rows], out.at[i, own_rows], od_ss.at[i], od_rs.at[i], core_peer
        )

    def out_to_chip(i):
        return remote(
            out.at[i, own_rows], out.at[i, own_rows], oi_ss.at[i], oi_rs.at[i], chip_peer
        )

    def out_forward(i):
        return remote(
            out.at[i, chip_rows], out.at[i, chip_rows], of_ss.at[i], of_rs.at[i], core_peer
        )

    def stage_g(i):
        sums_to_ffn(i).wait_recv()
        out[i, own_rows, :] = (
            resid[i].astype(F32)
            + (yk[i, 0:OW, :] + yrec[i, 0:OW, :].astype(F32) + yirec[i].astype(F32))
        ).astype(BF16)
        out_to_chip(i).start()
        out_to_core(i).start()

    def stage_h(i):
        out_to_chip(i).wait_recv()
        out_forward(i).start()

    def out_copy(i):
        return pltpu.make_async_copy(out.at[i], out_h.at[pl.ds(i * RW, RW)], out_sem.at[i])

    def finish(i):
        out_to_core(i).wait_recv()
        out_forward(i).wait_recv()
        out_copy(i).start()

    outw_copy.wait()
    fgain_copy.wait()

    def heads_step(i, _):
        stage_a(i)

        @pl.when(i > 0)
        def _sum():
            stage_b(i - 1)

        return _

    lax.fori_loop(0, CH, heads_step, 0)
    stage_b(CH - 1)
    stage_c(0)
    stage_c(1)
    exp_copy.wait()
    down_copy.wait()
    stage_d(0)
    stage_c(2)

    def ffn_step(i, _):
        stage_e_expand(i)

        @pl.when(i == 0)
        def _rows():
            stage_c(3)

        @pl.when(i < CH - 1)
        def _forward():
            stage_d(i + 1)

        @pl.when(i > 0)
        def _sum():
            stage_f(i - 1)

        @pl.when(i == CH - 1)
        def _output():
            stage_g(0)

        stage_e_down(i)
        return _

    lax.fori_loop(0, CH, ffn_step, 0)
    stage_g(1)
    stage_f(3)
    stage_h(0)
    stage_g(2)
    stage_h(1)
    finish(0)
    stage_g(3)
    stage_h(2)
    finish(1)
    stage_h(3)
    finish(2)
    finish(3)

    for d in range(1, PLANE):
        remote(ldsend, ld_in.at[0], ld_ss.at[d], ld_rs.at[d], core_peer).wait_send()
        remote(ssend.at[0], s_in.at[0], s_ss.at[d], s_rs.at[d], core_peer).wait_send()
        remote(isend.at[0], i_in.at[0], i_ss.at[d], i_rs.at[d], core_peer).wait_send()
    for d in range(1, DEPTH):
        remote(ltsend, lt_in.at[0], lt_ss.at[d], lt_rs.at[d], core_peer).wait_send()
        remote(tsend, t_in.at[0], t_ss.at[d], t_rs.at[d], core_peer).wait_send()
    for i in range(CH):
        for copy in (
            partial_to_core, partial_to_chip, rows_to_core, rows_to_ffn, rows_forward,
            sums_to_core, sums_to_ffn, out_to_core, out_to_chip, out_forward,
        ):
            copy(i).wait_send()
        out_copy(i).wait()


def local_layer(tokens, forget, attn_gain, projections, out_weight, ffn_gain, expand_weight, down_weight):
    dma = pltpu.SemaphoreType.DMA
    vmem = pltpu.VMEM
    scratch = [
        vmem((TOK, D), BF16),
        vmem((TOK, 8), F32),
        vmem((1, D), F32),
        vmem((1, D), F32),
        vmem((3, D, HD), BF16),
        vmem((HD, D), BF16),
        vmem((2, D, FF), BF16),
        vmem((FF, D), BF16),
        vmem((TOK, D), BF16),
        vmem((TOK, HD), BF16),
        vmem((TOK, HD), BF16),
        vmem((TOK, HD), BF16),
        vmem((TOK, 128), F32),
        vmem((8, 1, TOK), F32),
        vmem((TOK, HD), F32),
        vmem((TOK, HD), F32),
        vmem((8, 128), F32),
        vmem((PLANE, 8, 128), F32),
        vmem((8, 128), F32),
        vmem((DEPTH, 8, 128), F32),
        vmem((PLANE, 32, 128), BF16),
        vmem((PLANE, 32, 128), BF16),
        vmem((PLANE, 32, 128), F32),
        vmem((32, 128), BF16),
        vmem((DEPTH, 32, 128), BF16),
        vmem((PLANE, 32, 128), BF16),
        vmem((PLANE, 32, 128), BF16),
        vmem((NP, 128, 128), BF16),
        vmem((RW, HD), BF16),
        vmem((CH, 2 * OW, D), BF16),
        vmem((CH, 2 * OW, D), BF16),
        vmem((CH, 2 * OW, D), F32),
        vmem((CH, OW, D), BF16),
        vmem((CH, OW, D), BF16),
        vmem((CH, OW, D), BF16),
        vmem((CH, RW, D), BF16),
        vmem((RW, FF), BF16),
        vmem((CH, 2 * OW, D), BF16),
        vmem((CH, 2 * OW, D), BF16),
        vmem((CH, 2 * OW, D), F32),
        vmem((CH, OW, D), BF16),
        vmem((CH, OW, D), BF16),
        vmem((CH, RW, D), BF16),
        dma((CH,)),
        dma((9,)),
        dma((CH,)),
    ]
    scratch += [dma((8,)) for _ in range(10)]
    scratch += [dma((CH,)) for _ in range(20)]
    any_spec = pl.BlockSpec(memory_space=pl.ANY)
    return pl.pallas_call(
        kernel,
        out_shape=jax.ShapeDtypeStruct((TOK, D), BF16),
        in_specs=[any_spec] * 8,
        out_specs=any_spec,
        scratch_shapes=scratch,
        name="layer",
        compiler_params=pltpu.CompilerParams(
            collective_id=0, has_side_effects=True, vmem_limit_bytes=62 * 1024 * 1024
        ),
    )(
        tokens,
        forget,
        attn_gain.reshape(1, D),
        projections,
        out_weight,
        ffn_gain.reshape(1, D),
        expand_weight,
        down_weight,
    )


def solution(mesh):
    return jax.shard_map(
        local_layer,
        mesh=mesh,
        in_specs=(
            P("seq", None),
            P("seq", "tp"),
            P(),
            P(None, None, "tp"),
            P("tp", None),
            P(),
            P(None, None, "tp"),
            P("tp", None),
        ),
        out_specs=P("seq", None),
        check_vma=False,
    )
```

time: 251 us -> 74.4 us (0.30)
  blocking collectives: 134 us -> 0 us
  Pallas kernels: 0 us -> 69.6 us
  waiting for transfers between devices: 52.1 us -> 0 us
  matrix products: 39.7 us -> 0 us
  between operations: 13.6 us -> 0.01 us
  other arithmetic: 7 us -> 0 us
    all_to_all x3 -> x0, blocking collectives: 84.8 us -> none  [the longest x2 55.6 us: sent_to_all(): lax.all_to_all(jnp.broadcast_to(x[None], (peers, *x.shape)), axis, 0, 0,...]
    pallas_call x0 -> x1, Pallas kernels: none -> 69.6 us  [local_layer(): pl.pallas_call(kernel, out_shape=jax.ShapeDtypeStruct((TOK, D), BF16), in...]
    all_gather x5 -> x0, blocking collectives: 49.1 us -> none  [entering(): pieces = jax.tree.map(lambda part: lax.all_gather(part, axis), running)]
    dot_general x9 -> x0, matrix products: 39.7 us -> none  [the longest x3 10.6 us: local(): jnp.dot(normed, projections[which], preferred_element_type=jnp.float32)]
    reduce_scatter x1 -> x0, waiting for transfers between devices: 33.9 us -> none  [local(): lax.psum_scatter(jnp.dot(picked, out_weight, preferred_element_type=jnp.f...]
    all_gather x1 -> x0, waiting for transfers between devices: 18.2 us -> none  [entering(): pieces = jax.tree.map(lambda part: lax.all_gather(part, axis), running)]
    reduce_sum x3 -> x0, other arithmetic: 4.07 us -> none  [the longest x2 3.69 us: rms_scale(): mean_square = jnp.mean(widened * widened, axis=-1, keepdims=True)]
  transfers between devices with their start and end apart: 2 -> 0, of which waited for: 2 -> 0; matrix products, arithmetic and copies ran while one was open for 4% -> 0% of each run, Pallas kernels for 0% -> 0%
where the time goes in v1:
time: 74.4 us; the launch traced here: 74.3 us
  Pallas kernels  69.6 us (94%)
  local copies, waits for them, and re-layouts  4.71 us (6%)
    pallas_call x1, Pallas kernels, local_layer(): pl.pallas_call(kernel, out_shape=jax.ShapeDtypeStruct((TOK, D), BF16), in...  69.6 us
    unnamed x2, local copies, waits for them, and re-layouts  4.71 us

profile of v1, /device:TPU:1, one launch (start us, length us, event | category | flops | bytes accessed | tf_op | source)
XLA Modules:
  0.0 74.3 jit_solution(7599123494585388370)
XLA Ops:
  0.0 1.6 %copy.9.forget_h = f32[512,8]{1,0:T(8,128)} copy(f32[512,8]{0,1:T(8,128)} %param.9) | data formatting | bytes 32768 | tf_op args[1]
  1.6 69.6 %layer.1 = bf16[512,2048]{1,0:T(8,128)(2,1)} custom-call(bf16[512,2048]{1,0:T(8,128)(2,1)} %tok_h.1, f32[512,8]{1,0:T(8,128)} %copy.9.forget_h, f32[1,2048]{1,0:T(1,128)} %bitcast.2, bf16[3,2048,512]{2,1,0:T(8,128)(2,1)} %proj_h.1, bf16[512,2048]{1,0:T(8,128)(2,1)} %outw_h.1, f32[1,2048]{1,0:T(1,128)} %bitcast.3, bf16[2,2048,1024]{2,1,0:T(8,128)(2,1)} %exp_h.1, ...), custom_call_target="tpu_custom_call" | custom-call | tf_op jit(solution)/shard_map/layer/pallas_call | solution.py:553
  71.1 3.2 %copy.11 = bf16[512,2048]{1,0:T(8,128)(2,1)} copy(bf16[512,2048]{1,0:T(8,128)(2,1)} %layer.1) | data formatting | bytes 4194304

commit v2 on v1

--- a/solution.py
+++ b/solution.py
@@ -18,7 +18,10 @@
 D = 2048
 HD = 512
 FF = 1024
-CH = 4
+CH = 8
+EG = 2
+HG = 2
+AB = 128
 RW = TOK // CH
 OW = RW // 4
 NP = 4
@@ -26,18 +29,25 @@
 DEPTH = 8
 
 
+ORDER = (
+    "A0 A1 B0 B1", "B2 B3 A2 A3", "B5 C0 B4 B6", "C1 C2 C3 B7", "D0 C5 D1 C4", "D2 C6 X0 D3",
+    "C7 Y0 D5 X1", "D4 F1 F0 Y1", "D6 X2 D7 F2", "F3 Y2 X3 F4", "G1 Y3 G0 F5", "F6 G2 F7 G3",
+    "H1 G4 G5 G6", "G7 H2 H4 H5", "H3 Z4 H6 H0", "H7 Z1 Z3 Z5", "Z7 Z0 Z2 Z6",
+)
+
+
 def dot(a, b):
     return jnp.dot(a, b, preferred_element_type=F32)
 
 
 def kernel(
-    tok_h, forget_h, again_h, proj_h, outw_h, fgain_h, exp_h, down_h, out_h,
+    tok_h, forget_h, again_h, proj_h, outw_h, fgain_h, exp_h, down_h, out,
     tok, fgt, again, fgain, proj, outw, wexp, wdown,
     normed, qs, ks, vs, ld, ldt, ldx, local,
-    ldsend, ld_in, ltsend, lt_in, ssend, s_in, pref, tsend, t_in, isend, i_in, inc,
+    ldsend, ld_in, ltsend, lt_in, ssend, s_in, pref, carry, tsend, t_in, isend, i_in, inc,
     ho, psend, prec, pk, pisend, pirec,
-    resid, xrows, hidden, ysend, yrec, yk, yisend, yirec, out,
-    tok_sem, w_sem, out_sem,
+    resid, xrows, hidden, ysend, yrec, yk, yisend, yirec,
+    tok_sem, w_sem,
     ld_ss, ld_rs, lt_ss, lt_rs, s_ss, s_rs, t_ss, t_rs, i_ss, i_rs,
     p_ss, p_rs, pi_ss, pi_rs, xd_ss, xd_rs, xi_ss, xi_rs, xf_ss, xf_rs,
     y_ss, y_rs, yi_ss, yi_rs, od_ss, od_rs, oi_ss, oi_rs, of_ss, of_rs,
@@ -74,12 +84,9 @@
     for dev in (core_peer, chip_peer, ffn_peer):
         pl.semaphore_signal(barrier, inc=1, device_id=dev, device_id_type=MESH)
 
-    def tok_copy(i):
-        rows = pl.ds(i * RW, RW)
-        return pltpu.make_async_copy(tok_h.at[rows], tok.at[rows], tok_sem.at[i])
-
-    for i in range(CH):
-        tok_copy(i).start()
+    for i in range(TOK // AB):
+        rows = pl.ds(i * AB, AB)
+        pltpu.make_async_copy(tok_h.at[rows], tok.at[rows], tok_sem.at[i]).start()
     forget_copy = pltpu.make_async_copy(forget_h, fgt, w_sem.at[0])
     again_copy = pltpu.make_async_copy(again_h, again, w_sem.at[1])
     proj_copies = [
@@ -102,21 +109,20 @@
     f3 = (rest - f2.astype(F32)).astype(BF16)
     row_at = lax.broadcasted_iota(jnp.int32, (TOK, TOK), 0)
     col_at = lax.broadcasted_iota(jnp.int32, (TOK, TOK), 1)
-    lower = jnp.where(row_at >= col_at, 1.0, 0.0).astype(BF16)
-    sums = dot(lower, f1) + (dot(lower, f2) + dot(lower, f3))
-    ld[:, 0:8] = sums
-    ld[:, 8:128] = jnp.zeros((TOK, 120), F32)
-    turned = jnp.transpose(ld[...])
+    upper = jnp.where(row_at <= col_at, 1.0, 0.0).astype(BF16)
+    turned = dot(f1, upper) + (dot(f2, upper) + dot(f3, upper))
     for h in range(8):
         ldt[h] = turned[h : h + 1]
-    total = jnp.broadcast_to(turned[0:8, TOK - 1 : TOK], (8, 128))
-    ldsend[...] = total
-    ld_in[plane] = total
-
-    low_lanes = lax.broadcasted_iota(jnp.int32, (RW, 128), 1) < 64
-    for i in range(CH):
+    ld[...] = jnp.transpose(jnp.concatenate([turned, jnp.zeros((120, TOK), F32)], axis=0))
+    total = jnp.broadcast_to(turned[:, TOK - 1 : TOK], (8, 128))
+    for h in range(8):
+        ldsend[h] = total[h : h + 1]
+    ld_in[plane] = ldsend[plane]
+
+    low_lanes = lax.broadcasted_iota(jnp.int32, (AB, 128), 1) < 64
+    for i in range(TOK // AB):
         for p in range(NP):
-            rows = slice(i * RW, (i + 1) * RW)
+            rows = slice(i * AB, (i + 1) * AB)
             ldx[rows, p * 128 : (p + 1) * 128] = jnp.where(
                 low_lanes, ld[rows, 2 * p : 2 * p + 1], ld[rows, 2 * p + 1 : 2 * p + 2]
             )
@@ -125,27 +131,22 @@
 
     def norm_rows(i, _):
         pltpu.make_async_copy(
-            tok_h.at[pl.ds(i * RW, RW)], tok.at[pl.ds(i * RW, RW)], tok_sem.at[i]
+            tok_h.at[pl.ds(i * AB, AB)], tok.at[pl.ds(i * AB, AB)], tok_sem.at[i]
         ).wait()
-        rows = pl.ds(pl.multiple_of(i * RW, RW), RW)
+        rows = pl.ds(pl.multiple_of(i * AB, AB), AB)
         x = tok[rows, :].astype(F32)
         mean_square = jnp.sum(x * x, axis=1, keepdims=True) * (1.0 / D)
         scale = lax.rsqrt(mean_square + norm_epsilon)
         normed[rows, :] = (tok[rows, :].astype(F32) * scale * again[...]).astype(BF16)
         return _
 
-    lax.fori_loop(0, CH, norm_rows, 0)
+    lax.fori_loop(0, TOK // AB, norm_rows, 0)
 
     proj_copies[0].start()
     fgain_copy.start()
     outw_copy.start()
     exp_copy.start()
     down_copy.start()
-
-    pl.semaphore_wait(barrier, PLANE - 1 + DEPTH - 1 + 3)
-    for d in range(1, PLANE):
-        j, dev = plane_peer(d)
-        remote(ldsend, ld_in.at[plane], ld_ss.at[d], ld_rs.at[d], dev).start()
 
     proj_copies[1].wait()
     ks[...] = dot(normed[...], proj[1]).astype(BF16)
@@ -166,58 +167,60 @@
         ssend[2 * p + 1] = odd.astype(BF16)
 
     s_in[plane] = ssend[plane]
+    pl.semaphore_wait(barrier, PLANE - 1 + DEPTH - 1 + 3)
     for d in range(1, PLANE):
         j, dev = plane_peer(d)
         remote(ssend.at[j], s_in.at[plane], s_ss.at[d], s_rs.at[d], dev).start()
-
-    for d in range(1, PLANE):
-        remote(ldsend, ld_in.at[0], ld_ss.at[d], ld_rs.at[d], core_peer).wait_recv()
-    plane_total = ld_in[0]
-    for j in range(1, PLANE):
-        plane_total = plane_total + ld_in[j]
-    ltsend[...] = plane_total
-    lt_in[z] = plane_total
-    for d in range(1, DEPTH):
-        j, dev = depth_peer(d)
-        remote(ltsend, lt_in.at[z], lt_ss.at[d], lt_rs.at[d], dev).start()
+        remote(ldsend.at[j], ld_in.at[plane], ld_ss.at[d], ld_rs.at[d], dev).start()
 
     proj_copies[0].wait()
     qs[...] = (dot(normed[...], proj[0]) * 0.125).astype(BF16)
 
     def send_totals():
         for d in range(1, PLANE):
+            remote(ldsend.at[0], ld_in.at[0], ld_ss.at[d], ld_rs.at[d], core_peer).wait_recv()
             remote(ssend.at[0], s_in.at[0], s_ss.at[d], s_rs.at[d], core_peer).wait_recv()
+        passed = ld_in[0]
+        for j in range(1, PLANE):
+            passed = passed + ld_in[j]
+        ltsend[...] = passed
         state = jnp.zeros((32, 128), F32)
         for j in range(PLANE):
             pref[j] = state
-            state = jnp.exp(ld_in[j, pl.ds(plane, 1), :]) * state + s_in[j].astype(F32)
-        rounded = state.astype(BF16)
-        tsend[...] = rounded
-        t_in[z] = rounded
+            state = jnp.exp(ld_in[j]) * state + s_in[j].astype(F32)
+        tsend[...] = state.astype(BF16)
         for d in range(1, DEPTH):
-            j, dev = depth_peer(d)
-            remote(tsend, t_in.at[z], t_ss.at[d], t_rs.at[d], dev).start()
+
+            @pl.when(z + d < DEPTH)
+            def _later(d=d):
+                dev = ((z + d) * PLANE + plane, t)
+                remote(tsend, t_in.at[z], t_ss.at[d], t_rs.at[d], dev).start()
+                remote(ltsend, lt_in.at[z], lt_ss.at[d], lt_rs.at[d], dev).start()
 
     def send_prefixes():
-        for d in range(1, DEPTH):
-            remote(ltsend, lt_in.at[0], lt_ss.at[d], lt_rs.at[d], core_peer).wait_recv()
-            remote(tsend, t_in.at[0], t_ss.at[d], t_rs.at[d], core_peer).wait_recv()
-        state = jnp.zeros((32, 128), F32)
-        for j in range(DEPTH):
-            following = jnp.exp(lt_in[j, pl.ds(plane, 1), :]) * state + t_in[j].astype(F32)
-            state = jnp.where(j < z, following, state)
+        carry[...] = jnp.zeros((32, 128), F32)
+        for j in range(DEPTH - 1):
+
+            @pl.when(j < z)
+            def _earlier(j=j):
+                d = z - j
+                remote(ltsend, lt_in.at[j], lt_ss.at[d], lt_rs.at[d], core_peer).wait_recv()
+                remote(tsend, t_in.at[j], t_ss.at[d], t_rs.at[d], core_peer).wait_recv()
+                carry[...] = jnp.exp(lt_in[j]) * carry[...] + t_in[j].astype(F32)
+
+        state = carry[...]
         passed = jnp.zeros((1, 128), F32)
         for j in range(PLANE):
             isend[j] = (pref[j] + jnp.exp(passed) * state).astype(BF16)
-            passed = passed + ld_in[j, pl.ds(plane, 1), :]
+            passed = passed + ld_in[j]
         i_in[plane] = isend[plane]
         for d in range(1, PLANE):
             j, dev = plane_peer(d)
             remote(isend.at[j], i_in.at[plane], i_ss.at[d], i_rs.at[d], dev).start()
 
     lanes512 = lax.broadcasted_iota(jnp.int32, (TOK, 128), 1) < 64
-    causal = lax.broadcasted_iota(jnp.int32, (RW, RW), 0) >= lax.broadcasted_iota(
-        jnp.int32, (RW, RW), 1
+    causal = lax.broadcasted_iota(jnp.int32, (AB, AB), 0) >= lax.broadcasted_iota(
+        jnp.int32, (AB, AB), 1
     )
     zero = jnp.zeros((), BF16)
 
@@ -228,10 +231,10 @@
         for h in range(2):
             mine = lanes512 if h == 0 else jnp.logical_not(lanes512)
             vh = jnp.where(mine, vp.astype(F32), 0.0).astype(BF16)
-            for i in range(CH):
-                rows = slice(i * RW, (i + 1) * RW)
-                span = (i + 1) * RW
-                qh = jnp.where(mine[0:RW], qs[rows, cols].astype(F32), 0.0).astype(BF16)
+            for i in range(TOK // AB):
+                rows = slice(i * AB, (i + 1) * AB)
+                span = (i + 1) * AB
+                qh = jnp.where(mine[0:AB], qs[rows, cols].astype(F32), 0.0).astype(BF16)
                 scores = lax.dot_general(
                     qh, kp[0:span], (((1,), (1,)), ((), ())), preferred_element_type=F32
                 )
@@ -239,11 +242,11 @@
                 there = ldt[2 * p + h]
                 parts = []
                 for b in range(i + 1):
-                    gap = here - there[:, b * RW : (b + 1) * RW]
+                    gap = here - there[:, b * AB : (b + 1) * AB]
                     if b == i:
                         gap = jnp.where(causal, gap, -1e30)
                     parts.append(
-                        (scores[:, b * RW : (b + 1) * RW] * jnp.exp(gap)).astype(BF16)
+                        (scores[:, b * AB : (b + 1) * AB] * jnp.exp(gap)).astype(BF16)
                     )
                 weights = parts[0] if i == 0 else jnp.concatenate(parts, axis=1)
                 part = dot(weights, vh[0:span])
@@ -287,8 +290,8 @@
     def partial_to_chip(i):
         return remote(pisend.at[i], pirec.at[i], pi_ss.at[i], pi_rs.at[i], chip_peer)
 
-    def stage_a(i):
-        rows = pl.ds(pl.multiple_of(i * RW, RW), RW)
+    def stage_a(j):
+        rows = pl.ds(pl.multiple_of(j * HG * RW, HG * RW), HG * RW)
         for p in range(NP):
             cols = slice(p * 128, (p + 1) * 128)
             carried = dot(qs[rows, cols], inc[p])
@@ -298,18 +301,23 @@
             low = (square - high.astype(F32)).astype(BF16)
             mean_square = (dot(high, same_head) + dot(low, same_head)) * (1.0 / 64)
             headed = (attended * lax.rsqrt(mean_square + head_epsilon)).astype(BF16)
-            for kk in range(2):
-                core_slot = 1 - k if kk == 0 else k
-                for cc in range(2):
-                    chip_slot = c if cc == 0 else 1 - c
-                    at = pl.multiple_of(core_slot * 2 * OW + chip_slot * OW, OW)
-                    ho[pl.ds(at, OW), cols] = headed[(kk * 2 + cc) * OW : (kk * 2 + cc + 1) * OW]
+            for g in range(HG):
+                for kk in range(2):
+                    core_slot = 1 - k if kk == 0 else k
+                    for cc in range(2):
+                        chip_slot = c if cc == 0 else 1 - c
+                        at = pl.multiple_of(g * RW + core_slot * 2 * OW + chip_slot * OW, OW)
+                        first = g * RW + (kk * 2 + cc) * OW
+                        ho[pl.ds(at, OW), cols] = headed[first : first + OW]
         for n in range(4):
             cols = slice(n * 512, (n + 1) * 512)
             part = dot(ho[...], outw[:, cols])
-            psend[i, :, cols] = part[0 : 2 * OW].astype(BF16)
-            pk[i, :, cols] = part[2 * OW : 4 * OW]
-        partial_to_core(i).start()
+            for g in range(HG):
+                at = g * RW
+                psend[j * HG + g, :, cols] = part[at : at + 2 * OW].astype(BF16)
+                pk[j * HG + g, :, cols] = part[at + 2 * OW : at + 4 * OW]
+        for g in range(HG):
+            partial_to_core(j * HG + g).start()
 
     def stage_b(i):
         partial_to_core(i).wait_recv()
@@ -361,23 +369,27 @@
     def sums_to_ffn(i):
         return remote(yisend.at[i], yirec.at[i], yi_ss.at[i], yi_rs.at[i], ffn_peer)
 
-    def stage_e_expand(i):
-        rows_to_core(i).wait_recv()
-        rows_forward(i).wait_recv()
-        x = xrows.at[i]
+    def stage_x(j):
+        for g in range(EG):
+            rows_to_core(j * EG + g).wait_recv()
+            rows_forward(j * EG + g).wait_recv()
+        x = xrows[pl.ds(j * EG, EG)].reshape(EG * RW, D)
         for n in range(4):
             cols = slice(n * 256, (n + 1) * 256)
-            gate = dot(x[...], wexp[0, :, cols])
-            up = dot(x[...], wexp[1, :, cols])
+            gate = dot(x, wexp[0, :, cols])
+            up = dot(x, wexp[1, :, cols])
             hidden[:, cols] = (gate / (1.0 + jnp.exp(-gate)) * up).astype(BF16)
 
-    def stage_e_down(i):
+    def stage_y(j):
         for n in range(4):
             cols = slice(n * 512, (n + 1) * 512)
             part = dot(hidden[...], wdown[:, cols])
-            ysend[i, :, cols] = part[0 : 2 * OW].astype(BF16)
-            yk[i, :, cols] = part[2 * OW : 4 * OW]
-        sums_to_core(i).start()
+            for g in range(EG):
+                at = g * RW
+                ysend[j * EG + g, :, cols] = part[at : at + 2 * OW].astype(BF16)
+                yk[j * EG + g, :, cols] = part[at + 2 * OW : at + 4 * OW]
+        for g in range(EG):
+            sums_to_core(j * EG + g).start()
 
     def stage_f(i):
         sums_to_core(i).wait_recv()
@@ -415,85 +427,76 @@
         out_to_chip(i).wait_recv()
         out_forward(i).start()
 
-    def out_copy(i):
-        return pltpu.make_async_copy(out.at[i], out_h.at[pl.ds(i * RW, RW)], out_sem.at[i])
-
-    def finish(i):
+    def stage_z(i):
         out_to_core(i).wait_recv()
         out_forward(i).wait_recv()
-        out_copy(i).start()
 
     outw_copy.wait()
     fgain_copy.wait()
+    stages = {
+        "A": stage_a, "B": stage_b, "C": stage_c, "D": stage_d, "X": stage_x,
+        "Y": stage_y, "F": stage_f, "G": stage_g, "H": stage_h, "Z": stage_z,
+    }
+    ops = [(word[0], int(word[1:])) for part in ORDER for word in part.split()]
+
+    def run(some):
+        for name, i in some:
+            stages[name](i)
+
+    def between(first, last):
+        start = ops.index(first) + 1
+        return ops[start : ops.index(last)] if last in ops else ops[start:]
+
+    def guarded(step, lists):
+        for i, some in enumerate(lists):
+            if some:
+                pl.when(step == i)(functools.partial(run, some))
+
+    groups = CH // HG
+    after_a = [between(("A", j), ("A", j + 1)) for j in range(groups - 1)]
+    middle = between(("A", groups - 1), ("X", 0))
+    steps = CH // EG
+    inside = [between(("X", j), ("Y", j)) for j in range(steps)]
+    after_y = [between(("Y", j), ("X", j + 1)) for j in range(steps - 1)]
+    tail = between(("Y", steps - 1), None)
 
     def heads_step(i, _):
         stage_a(i)
-
-        @pl.when(i > 0)
-        def _sum():
-            stage_b(i - 1)
-
+        guarded(i, after_a)
         return _
 
-    lax.fori_loop(0, CH, heads_step, 0)
-    stage_b(CH - 1)
-    stage_c(0)
-    stage_c(1)
+    lax.fori_loop(0, groups, heads_step, 0)
+    run(middle)
     exp_copy.wait()
     down_copy.wait()
-    stage_d(0)
-    stage_c(2)
-
-    def ffn_step(i, _):
-        stage_e_expand(i)
-
-        @pl.when(i == 0)
-        def _rows():
-            stage_c(3)
-
-        @pl.when(i < CH - 1)
-        def _forward():
-            stage_d(i + 1)
-
-        @pl.when(i > 0)
-        def _sum():
-            stage_f(i - 1)
-
-        @pl.when(i == CH - 1)
-        def _output():
-            stage_g(0)
-
-        stage_e_down(i)
+
+    def ffn_step(j, _):
+        stage_x(j)
+        guarded(j, inside)
+        stage_y(j)
+        guarded(j, after_y)
         return _
 
-    lax.fori_loop(0, CH, ffn_step, 0)
-    stage_g(1)
-    stage_f(3)
-    stage_h(0)
-    stage_g(2)
-    stage_h(1)
-    finish(0)
-    stage_g(3)
-    stage_h(2)
-    finish(1)
-    stage_h(3)
-    finish(2)
-    finish(3)
+    lax.fori_loop(0, steps, ffn_step, 0)
+    run(tail)
 
     for d in range(1, PLANE):
-        remote(ldsend, ld_in.at[0], ld_ss.at[d], ld_rs.at[d], core_peer).wait_send()
+        remote(ldsend.at[0], ld_in.at[0], ld_ss.at[d], ld_rs.at[d], core_peer).wait_send()
         remote(ssend.at[0], s_in.at[0], s_ss.at[d], s_rs.at[d], core_peer).wait_send()
         remote(isend.at[0], i_in.at[0], i_ss.at[d], i_rs.at[d], core_peer).wait_send()
     for d in range(1, DEPTH):
-        remote(ltsend, lt_in.at[0], lt_ss.at[d], lt_rs.at[d], core_peer).wait_send()
-        remote(tsend, t_in.at[0], t_ss.at[d], t_rs.at[d], core_peer).wait_send()
+
+        @pl.when(z + d < DEPTH)
+        def _sent(d=d):
+            remote(ltsend, lt_in.at[0], lt_ss.at[d], lt_rs.at[d], core_peer).wait_send()
+            remote(tsend, t_in.at[0], t_ss.at[d], t_rs.at[d], core_peer).wait_send()
+
     for i in range(CH):
         for copy in (
             partial_to_core, partial_to_chip, rows_to_core, rows_to_ffn, rows_forward,
             sums_to_core, sums_to_ffn, out_to_core, out_to_chip, out_forward,
         ):
             copy(i).wait_send()
-        out_copy(i).wait()
 
 
 def local_layer(tokens, forget, attn_gain, projections, out_weight, ffn_gain, expand_weight, down_weight):
@@ -501,7 +504,7 @@
     vmem = pltpu.VMEM
     scratch = [
         vmem((TOK, D), BF16),
-        vmem((TOK, 8), F32),
+        vmem((8, TOK), F32),
         vmem((1, D), F32),
         vmem((1, D), F32),
         vmem((3, D, HD), BF16),
@@ -516,19 +519,20 @@
         vmem((8, 1, TOK), F32),
         vmem((TOK, HD), F32),
         vmem((TOK, HD), F32),
-        vmem((8, 128), F32),
-        vmem((PLANE, 8, 128), F32),
-        vmem((8, 128), F32),
-        vmem((DEPTH, 8, 128), F32),
+        vmem((PLANE, 1, 128), F32),
+        vmem((PLANE, 1, 128), F32),
+        vmem((1, 128), F32),
+        vmem((DEPTH, 1, 128), F32),
         vmem((PLANE, 32, 128), BF16),
         vmem((PLANE, 32, 128), BF16),
         vmem((PLANE, 32, 128), F32),
+        vmem((32, 128), F32),
         vmem((32, 128), BF16),
         vmem((DEPTH, 32, 128), BF16),
         vmem((PLANE, 32, 128), BF16),
         vmem((PLANE, 32, 128), BF16),
         vmem((NP, 128, 128), BF16),
-        vmem((RW, HD), BF16),
+        vmem((HG * RW, HD), BF16),
         vmem((CH, 2 * OW, D), BF16),
         vmem((CH, 2 * OW, D), BF16),
         vmem((CH, 2 * OW, D), F32),
@@ -536,33 +540,31 @@
         vmem((CH, OW, D), BF16),
         vmem((CH, OW, D), BF16),
         vmem((CH, RW, D), BF16),
-        vmem((RW, FF), BF16),
+        vmem((EG * RW, FF), BF16),
         vmem((CH, 2 * OW, D), BF16),
         vmem((CH, 2 * OW, D), BF16),
         vmem((CH, 2 * OW, D), F32),
         vmem((CH, OW, D), BF16),
         vmem((CH, OW, D), BF16),
-        vmem((CH, RW, D), BF16),
-        dma((CH,)),
+        dma((TOK // AB,)),
         dma((9,)),
-        dma((CH,)),
     ]
     scratch += [dma((8,)) for _ in range(10)]
     scratch += [dma((CH,)) for _ in range(20)]
     any_spec = pl.BlockSpec(memory_space=pl.ANY)
-    return pl.pallas_call(
+    result = pl.pallas_call(
         kernel,
-        out_shape=jax.ShapeDtypeStruct((TOK, D), BF16),
+        out_shape=vmem((CH, RW, D), BF16),
         in_specs=[any_spec] * 8,
-        out_specs=any_spec,
+        out_specs=pl.BlockSpec(memory_space=vmem),
         scratch_shapes=scratch,
         name="layer",
         compiler_params=pltpu.CompilerParams(
-            collective_id=0, has_side_effects=True, vmem_limit_bytes=62 * 1024 * 1024
+            collective_id=0, has_side_effects=True, vmem_limit_bytes=58 * 1024 * 1024
         ),
     )(
         tokens,
-        forget,
+        forget.T,
         attn_gain.reshape(1, D),
         projections,
         out_weight,
@@ -570,6 +572,7 @@
         expand_weight,
         down_weight,
     )
+    return result.reshape(TOK, D)
 
 
 def solution(mesh):

time: 74.4 us -> 63.4 us (0.85)
  Pallas kernels: 69.6 us -> 62 us
  local copies, waits for them, and re-layouts: 4.71 us -> 1.32 us
    pallas_call x1, Pallas kernels: 69.6 us -> 62 us  [local_layer(): pl.pallas_call(kernel, out_shape=vmem((CH, RW, D), BF16), in_specs=[any_s...]
    unnamed x2 -> x1, local copies, waits for them, and re-layouts: 4.71 us -> 1.32 us
where the time goes in v2:
time: 63.4 us; the launch traced here: 63.3 us
  Pallas kernels  62 us (98%)
  local copies, waits for them, and re-layouts  1.32 us (2%)
    pallas_call x1, Pallas kernels, local_layer(): pl.pallas_call(kernel, out_shape=vmem((CH, RW, D), BF16), in_specs=[any_s...  62 us
    unnamed x1, local copies, waits for them, and re-layouts  1.32 us

profile of v2, /device:TPU:1, one launch (start us, length us, event | category | flops | bytes accessed | tf_op | source)
XLA Modules:
  0.0 63.3 jit_solution(2626460762284014597)
XLA Ops:
  0.0 62.0 %layer.1 = bf16[8,64,2048]{2,1,0:T(8,128)(2,1)S(1)} custom-call(bf16[512,2048]{1,0:T(8,128)(2,1)} %tok_h.1, f32[8,512]{1,0:T(8,128)} %bitcast.5, f32[1,2048]{1,0:T(1,128)} %bitcast.6, bf16[3,2048,512]{2,1,0:T(8,128)(2,1)} %proj_h.1, bf16[512,2048]{1,0:T(8,128)(2,1)} %outw_h.1, f32[1,2048]{1,0:T(1,128)} %bitcast.7, bf16[2,2048,1024]{2,1,0:T(8,128)(2,1)} %exp_h.1, ...), custom_call_target="tpu_custom_call" | custom-call | tf_op jit(solution)/shard_map/layer/pallas_call | solution.py:555
  62.0 1.3 %copy.10 = bf16[512,2048]{1,0:T(8,128)(2,1)} copy(bf16[512,2048]{1,0:T(8,128)(2,1)S(1)} %bitcast.4) | data formatting | bytes 4194304

commit v3 on v2

--- a/solution.py
+++ b/solution.py
@@ -27,6 +27,7 @@
 NP = 4
 PLANE = 8
 DEPTH = 8
+FAR_FIRST = (4, 3, 5, 2, 6, 1, 7)
 
 
 ORDER = (
@@ -168,9 +169,11 @@
 
     s_in[plane] = ssend[plane]
     pl.semaphore_wait(barrier, PLANE - 1 + DEPTH - 1 + 3)
-    for d in range(1, PLANE):
+    for d in FAR_FIRST:
         j, dev = plane_peer(d)
         remote(ssend.at[j], s_in.at[plane], s_ss.at[d], s_rs.at[d], dev).start()
+    for d in FAR_FIRST:
+        j, dev = plane_peer(d)
         remote(ldsend.at[j], ld_in.at[plane], ld_ss.at[d], ld_rs.at[d], dev).start()
 
     proj_copies[0].wait()
@@ -189,7 +192,7 @@
             pref[j] = state
             state = jnp.exp(ld_in[j]) * state + s_in[j].astype(F32)
         tsend[...] = state.astype(BF16)
-        for d in range(1, DEPTH):
+        for d in FAR_FIRST:
 
             @pl.when(z + d < DEPTH)
             def _later(d=d):
@@ -214,7 +217,7 @@
             isend[j] = (pref[j] + jnp.exp(passed) * state).astype(BF16)
             passed = passed + ld_in[j]
         i_in[plane] = isend[plane]
-        for d in range(1, PLANE):
+        for d in FAR_FIRST:
             j, dev = plane_peer(d)
             remote(isend.at[j], i_in.at[plane], i_ss.at[d], i_rs.at[d], dev).start()
 

time: 63.4 us -> 63.4 us (level)
  no operation moved by 1% of the time
where the time goes in v3:
time: 63.4 us; the launch traced here: 63.3 us
  Pallas kernels  62 us (98%)
  local copies, waits for them, and re-layouts  1.32 us (2%)
    pallas_call x1, Pallas kernels, local_layer(): pl.pallas_call(kernel, out_shape=vmem((CH, RW, D), BF16), in_specs=[any_s...  62 us
    unnamed x1, local copies, waits for them, and re-layouts  1.32 us

profile of v3, /device:TPU:1, one launch (start us, length us, event | category | flops | bytes accessed | tf_op | source)
XLA Modules:
  0.0 63.3 jit_solution(7006861868272518173)
XLA Ops:
  0.0 62.0 %layer.1 = bf16[8,64,2048]{2,1,0:T(8,128)(2,1)S(1)} custom-call(bf16[512,2048]{1,0:T(8,128)(2,1)} %tok_h.1, f32[8,512]{1,0:T(8,128)} %bitcast.5, f32[1,2048]{1,0:T(1,128)} %bitcast.6, bf16[3,2048,512]{2,1,0:T(8,128)(2,1)} %proj_h.1, bf16[512,2048]{1,0:T(8,128)(2,1)} %outw_h.1, f32[1,2048]{1,0:T(1,128)} %bitcast.7, bf16[2,2048,1024]{2,1,0:T(8,128)(2,1)} %exp_h.1, ...), custom_call_target="tpu_custom_call" | custom-call | tf_op jit(solution)/shard_map/layer/pallas_call | solution.py:558
  62.0 1.3 %copy.10 = bf16[512,2048]{1,0:T(8,128)(2,1)} copy(bf16[512,2048]{1,0:T(8,128)(2,1)S(1)} %bitcast.4) | data formatting | bytes 4194304
